TPU v7x, 256 devices: a 2x2x32 block of a 4x8x32 slice. The times are simulated.
256 devices in a mesh: groups: 4 (over x, y), space: 64 (over z, core).
Axes of the slice: x: 2, y: 2, z: 32, core: 2. Of those that a mesh axis runs over, the one named last changes fastest.
The devices are a block of a 4x8x32 slice.
Arguments:
- inputs: bfloat16 [1536, 1152, 256], P(('groups', 'space')), parts along dimension 0, may hold values from -6 to 6
- spectral_weight: bfloat16 [2, 256, 2, 256, 256], P(None, 'space'), may hold values from -0.25 to 0.25
- local_weight: bfloat16 [2, 256, 256], replicated, may hold values from -0.375 to 0.375
- layer_bias: bfloat16 [2, 256], replicated, may hold values from -3 to 3
- readout_hidden: bfloat16 [256, 256], replicated, may hold values from -0.375 to 0.375
- readout_final: bfloat16 [20, 256], replicated, may hold values from -0.375 to 0.375
Outputs:
- forecast: bfloat16 [20, 1536, 1152], P(None, ('groups', 'space')), parts along dimension 1
There are 4 independent parts, one for each index of `groups`. A program takes and returns all parts, laid end to end along the dimension named above; an argument that names none is the same for every part. Nothing has to cross between parts.
All inputs are finite; a program needn't handle non-finite values.
Results may differ from a plain program's by a relative error of at most 0.018.
Values may be sent and summed in bfloat16 or wider, within the bound.
A program may use at most 64 MiB of HBM per device.

v0:
```python
import jax
import jax.numpy as jnp
from jax import lax
from jax.sharding import PartitionSpec as P

KY = 16
KX = 16
LAYERS = 2
MODES = 256


def in_blocks(value, dim, peers):
    shape = value.shape
    blocks = value.reshape(*shape[:dim], peers, shape[dim] // peers, *shape[dim + 1 :])
    return jnp.moveaxis(blocks, dim, 0)


def sent_and_summed(value, axis, dim):
    peers = lax.axis_size(axis)
    blocks = lax.all_to_all(in_blocks(value, dim, peers), axis, 0, 0, tiled=True)
    return jnp.sum(blocks.astype(jnp.float32), axis=0)


def joined_along(blocks, dim):
    shape = list(blocks.shape[1:])
    shape[dim] *= blocks.shape[0]
    return jnp.moveaxis(blocks, 0, dim).reshape(shape)


def from_everyone(value, axis):
    peers = lax.axis_size(axis)
    return lax.all_to_all(
        jnp.broadcast_to(value[None], (peers, *value.shape)), axis, 0, 0, tiled=True
    )


def collect(value, axis, dim):
    return joined_along(from_everyone(value, axis), dim)


def zonal_tables(columns, modes):
    column_ids = jnp.arange(columns, dtype=jnp.int32)
    wave_numbers = jnp.arange(1, modes + 1, dtype=jnp.int32)
    phase_int = column_ids[:, None] * wave_numbers[None, :] % columns
    angles = 2.0 * jnp.pi / columns * phase_int.astype(jnp.float32)
    cosines = jnp.cos(angles)
    sines = jnp.sin(angles)
    forward = jnp.concatenate([cosines, -sines], axis=1) / jnp.sqrt(jnp.float32(columns))
    inverse = jnp.stack([cosines, -sines], axis=2).reshape(columns, 2 * modes) * jnp.sqrt(
        jnp.float32(2.0 / modes)
    )
    return (forward.astype(jnp.bfloat16), inverse.astype(jnp.bfloat16))


def meridional_tables(row_ids, height, modes):
    mode_index = jnp.arange(modes, dtype=jnp.int32)
    wave_numbers = jnp.where(mode_index < modes // 2, mode_index, mode_index - modes)
    phase_int = wave_numbers[:, None] * row_ids[None, :] % height
    angles = 2.0 * jnp.pi / height * phase_int.astype(jnp.float32)
    cosines = jnp.cos(angles)
    sines = jnp.sin(angles)
    forward = jnp.stack(
        [jnp.stack([cosines, sines], axis=2), jnp.stack([-sines, cosines], axis=2)], axis=1
    )
    forward = forward / jnp.sqrt(jnp.float32(height))
    cos_rows = cosines.T
    sin_rows = sines.T
    inverse = jnp.stack(
        [jnp.stack([cos_rows, -sin_rows], axis=2), jnp.stack([sin_rows, cos_rows], axis=2)], axis=1
    )
    inverse = inverse / jnp.sqrt(jnp.float32(modes))
    return (forward.astype(jnp.bfloat16), inverse.astype(jnp.bfloat16))


def mix_modes(spectrum, weights):
    real_in = spectrum[:, 0]
    imag_in = spectrum[:, 1]
    real_weight = weights[:, 0]
    imag_weight = weights[:, 1]

    def product(vectors, matrices):
        return jnp.einsum("mi,mio->mo", vectors, matrices, preferred_element_type=jnp.float32)

    real_out = product(real_in, real_weight) - product(imag_in, imag_weight)
    imag_out = product(real_in, imag_weight) + product(imag_in, real_weight)
    return jnp.stack([real_out, imag_out], axis=1).astype(jnp.bfloat16)


def per_device(inputs, spectral_weight, local_weight, layer_bias, readout_hidden, readout_final):
    rows_here, columns, channels = inputs.shape
    devices_along = lax.axis_size("space")
    height = rows_here * devices_along
    zonal_forward, zonal_inverse = zonal_tables(columns, KX)
    local_rows = jnp.arange(rows_here, dtype=jnp.int32) * devices_along + lax.axis_index("space")
    forward_here, inverse_here = meridional_tables(local_rows, height, KY)
    current = inputs
    for layer_index in range(LAYERS):
        zonal_part = jnp.einsum(
            "hwc,wj->hjc", current, zonal_forward, preferred_element_type=jnp.float32
        )
        zonal_view = zonal_part.astype(jnp.bfloat16).reshape(rows_here, 2, KX, channels)
        partial_value = jnp.einsum(
            "qphr,hrkc->qkpc", forward_here, zonal_view, preferred_element_type=jnp.float32
        )
        partial_value = partial_value.reshape(MODES, 2 * channels)
        spectrum = sent_and_summed(partial_value.astype(jnp.bfloat16), "space", 0).reshape(
            -1, 2, channels
        )
        mixed = mix_modes(spectrum.astype(jnp.bfloat16), spectral_weight[layer_index])
        all_modes = collect(mixed, "space", 0).reshape(KY, KX, 2, channels)
        returned = jnp.einsum(
            "hpqr,qkrc->hkpc", inverse_here, all_modes, preferred_element_type=jnp.float32
        )
        returned = returned.astype(jnp.bfloat16).reshape(rows_here, 2 * KX, channels)
        spread = jnp.einsum(
            "wj,hjc->hwc", zonal_inverse, returned, preferred_element_type=jnp.float32
        )
        pointwise = jnp.dot(
            current.reshape(-1, channels),
            local_weight[layer_index],
            preferred_element_type=jnp.float32,
        )
        pointwise = pointwise.reshape(current.shape)
        bias_now = layer_bias[layer_index].astype(jnp.float32)
        current = jax.nn.gelu(spread + pointwise + bias_now, approximate=True).astype(jnp.bfloat16)
    hidden = jnp.dot(
        current.reshape(-1, channels), readout_hidden, preferred_element_type=jnp.float32
    )
    hidden = jax.nn.gelu(hidden, approximate=True).astype(jnp.bfloat16)
    final = jnp.einsum("pq,nq->pn", readout_final, hidden, preferred_element_type=jnp.float32)
    return final.astype(jnp.bfloat16).reshape(readout_final.shape[0], rows_here, columns)


def solution(mesh):
    in_specs = (
        P(("groups", "space"), None, None),
        P(None, "space", None, None, None),
        P(),
        P(),
        P(),
        P(),
    )
    out_specs = P(None, ("groups", "space"), None)
    return jax.shard_map(
        per_device, mesh=mesh, in_specs=in_specs, out_specs=out_specs, check_vma=False
    )
```

profile of v0, /device:TPU:37, one launch (start us, length us, event | category | flops | bytes accessed | tf_op | source)
XLA Modules:
  0.0 278.1 jit_solution(9218066294072171287)
XLA Ops:
  0.0 0.0 copy-start
  0.0 0.0 copy-start.8
  0.0 0.0 copy-start.9
  0.1 0.4 fusion.69
  0.4 0.0 copy-start.3
  0.5 0.0 copy-start.5
  0.5 0.1 fusion.88
  0.6 0.0 copy-done.7
  0.6 0.0 copy-done.8
  0.6 0.0 copy-done.9
  0.6 1.4 copy-done
  2.1 0.7 convolution_convert_fusion.2
  2.8 0.0 copy-done.3
  2.8 0.0 copy-done.5
  2.8 0.3 fusion.31
  3.1 0.9 copy.82
  4.0 1.8 convert_element_type.178
  5.8 34.3 %all-to-all-start = ((bf16[64,4,512]{2,1,0:T(4,128)(2,1)}), bf16[64,4,512]{2,1,0:T(4,128)(2,1)}, u32[]{:S(2)}, u32[]{:S(2)}) async-start(bf16[64,4,512]{2,1,0:T(4,128)(2,1)} %convert_element_type.178), calls=%async_computation | async-start | bytes 524288 | tf_op jit(solution)/shard_map/all_to_all | solution.py:20
  40.2 3.1 %slice_bitcast_fusion.1 = (bf16[4,2,256,256]{3,2,1,0:T(8,128)(2,1)}, bf16[4,2,256,256]{3,2,1,0:T(8,128)(2,1)}) fusion(bf16[2,4,2,256,256]{4,3,2,1,0:T(8,128)(2,1)} %param.7), kind=kLoop, calls=%fused_computation.48 | loop fusion | bytes 4194304 | tf_op jit(solution)/shard_map/squeeze | solution.py:109
  43.3 38.2 %all-to-all-done = bf16[64,4,512]{2,1,0:T(4,128)(2,1)} async-done(((bf16[64,4,512]{2,1,0:T(4,128)(2,1)}), bf16[64,4,512]{2,1,0:T(4,128)(2,1)}, u32[]{:S(2)}, u32[]{:S(2)}) %all-to-all-start) | async-done | bytes 262176 | tf_op jit(solution)/shard_map/all_to_all | solution.py:20
  81.4 1.7 reduce_sum.24
  83.1 0.7 slice_bitcast_fusion.17
  83.8 1.2 fusion.38
  85.0 1.2 fusion.37
  86.3 1.2 fusion.36
  87.5 1.2 fusion.39
  88.7 0.8 broadcast_in_dim.4
  89.6 7.4 %all-to-all-start.1 = ((bf16[64,4,2,256]{3,2,1,0:T(2,128)(2,1)}), bf16[64,4,2,256]{3,2,1,0:T(2,128)(2,1)}, u32[]{:S(2)}, u32[]{:S(2)}) async-start(bf16[64,4,2,256]{3,2,1,0:T(2,128)(2,1)} %broadcast_in_dim.4), calls=%async_computation.1 | async-start | bytes 524288 | tf_op jit(solution)/shard_map/all_to_all | solution.py:32
  97.0 0.8 fusion.132
  97.8 1.3 slice_convert_fusion
  99.1 0.6 copy_bitcast_fusion
  99.7 1.7 fusion.66
  101.5 38.2 %all-to-all-done.1 = bf16[64,4,2,256]{3,2,1,0:T(2,128)(2,1)} async-done(((bf16[64,4,2,256]{3,2,1,0:T(2,128)(2,1)}), bf16[64,4,2,256]{3,2,1,0:T(2,128)(2,1)}, u32[]{:S(2)}, u32[]{:S(2)}) %all-to-all-start.1) | async-done | bytes 262176 | tf_op jit(solution)/shard_map/all_to_all | solution.py:32
  139.7 1.3 fusion.35
  141.0 2.1 fusion.56
  143.0 0.0 copy-done.11
  143.0 0.0 copy-done.12
  143.1 0.0 copy-start.4
  143.1 0.0 copy-start.6
  143.1 3.4 %fusion.8 = bf16[6,1152,256]{1,2,0:T(8,128)(2,1)S(1)} fusion(f32[6,256,1152,1]{2,1,3,0:T(8,128)S(1)} %fusion.56, bf16[6,1152,256]{2,1,0:T(8,128)(2,1)S(1)} %copy-done, f32[256]{0:T(256)S(1)} %bitcast.203, bf16[2,256,256]{2,1,0:T(8,128)(2,1)S(1)} %copy-done.12), kind=kOutput, calls=%fused_computation.12 | convolution fusion | flops 925433856 | bytes 14287872 | tf_op jit(solution)/shard_map/dot_general | solution.py:118
  146.5 0.0 copy-start.1
  146.5 1.7 copy-done.1
  148.2 0.0 copy-done.4
  148.2 0.0 copy-done.6
  148.2 1.1 convolution_convert_fusion.1
  149.4 0.3 fusion.30
  149.7 0.9 copy.91
  150.6 1.8 convert_element_type.193
  152.4 49.1 %all_to_all.20 = bf16[64,4,512]{2,1,0:T(4,128)(2,1)} all-to-all(bf16[64,4,512]{2,1,0:T(4,128)(2,1)} %convert_element_type.193), channel_id=1, replica_groups=mesh['groups'=4,'space'=64] {'space'}, dimensions={0} | all-to-all | bytes 524288 | tf_op jit(solution)/shard_map/all_to_all | solution.py:20
  201.6 1.1 reduce_sum.25
  202.7 1.2 fusion.42
  203.9 1.2 fusion.41
  205.1 1.2 fusion.40
  206.4 1.4 fusion.43
  207.8 0.1 broadcast_in_dim.5
  207.9 47.4 %all_to_all.21 = bf16[64,4,2,256]{3,2,1,0:T(2,128)(2,1)S(1)} all-to-all(bf16[64,4,2,256]{3,2,1,0:T(2,128)(2,1)S(1)} %broadcast_in_dim.5), channel_id=1, replica_groups=mesh['groups'=4,'space'=64] {'space'}, dimensions={0} | all-to-all | bytes 524288 | tf_op jit(solution)/shard_map/all_to_all | solution.py:32
  255.3 1.0 fusion.34
  256.3 2.1 fusion.54
  258.4 0.0 copy-done.2
  258.4 4.9 %fusion.16 = bf16[6,1152,256]{1,2,0:T(8,128)(2,1)} fusion(f32[6,256,1152,1]{2,1,3,0:T(8,128)S(1)} %fusion.54, bf16[6,1152,256]{1,2,0:T(8,128)(2,1)S(1)} %copy-done.2, f32[256]{0:T(256)S(1)} %bitcast.202, bf16[2,256,256]{2,1,0:T(8,128)(2,1)S(1)} %copy-done.13), kind=kOutput, calls=%fused_computation.20 | convolution fusion | flops 925433856 | bytes 14287872 | tf_op jit(solution)/shard_map/dot_general | solution.py:118
  263.3 5.8 %copy.97 = bf16[6,1152,256]{2,1,0:T(8,128)(2,1)} copy(bf16[6,1152,256]{1,2,0:T(8,128)(2,1)} %fusion.16) | data formatting | bytes 7077888 | tf_op jit(solution)/shard_map/convert_element_type | solution.py:125
  269.1 5.2 %fusion = bf16[20,6912]{1,0:T(8,128)(2,1)} fusion(bf16[20,256]{1,0:T(8,128)(2,1)S(1)} %copy-done.14, bf16[6912,256]{1,0:T(8,128)(2,1)} %bitcast.196, bf16[256,256]{1,0:T(8,128)(2,1)} %param.10), kind=kOutput, calls=%fused_computation.4 | convolution fusion | flops 992812032 | bytes 3956736 | tf_op jit(solution)/shard_map/pq,nq->pn/dot_general | solution.py:130
  274.3 2.1 reshape.503
  276.4 1.7 copy.98
  (23 shorter events, 0.1 us)
Async XLA Ops:
  0.0 2.1 copy-start
  0.0 0.6 copy-start.7
  0.0 0.6 copy-start.8
  0.0 0.6 copy-start.9
  0.4 2.3 copy-start.3
  0.5 2.3 copy-start.5
  5.8 75.6 %all-to-all-start = ((bf16[64,4,512]{2,1,0:T(4,128)(2,1)}), bf16[64,4,512]{2,1,0:T(4,128)(2,1)}, u32[]{:S(2)}, u32[]{:S(2)}) async-start(bf16[64,4,512]{2,1,0:T(4,128)(2,1)} %convert_element_type.178), calls=%async_computation | async-start | bytes 524288 | tf_op jit(solution)/shard_map/all_to_all | solution.py:20
  89.6 50.1 %all-to-all-start.1 = ((bf16[64,4,2,256]{3,2,1,0:T(2,128)(2,1)}), bf16[64,4,2,256]{3,2,1,0:T(2,128)(2,1)}, u32[]{:S(2)}, u32[]{:S(2)}) async-start(bf16[64,4,2,256]{3,2,1,0:T(2,128)(2,1)} %broadcast_in_dim.4), calls=%async_computation.1 | async-start | bytes 524288 | tf_op jit(solution)/shard_map/all_to_all | solution.py:32
  139.7 3.4 %copy-start.11 = (f32[1,256]{1,0:T(1,128)S(1)}, f32[1,256]{1,0:T(1,128)}, u32[]{:S(2)}) copy-start(f32[1,256]{1,0:T(1,128)} %get-tuple-element.18) | copy-start | bytes 3076
  139.7 3.4 %copy-start.12 = (bf16[2,256,256]{2,1,0:T(8,128)(2,1)S(1)}, bf16[2,256,256]{2,1,0:T(8,128)(2,1)}, u32[]{:S(2)}) copy-start(bf16[2,256,256]{2,1,0:T(8,128)(2,1)} %param.8) | copy-start | bytes 786436
  143.1 5.2 %copy-start.4 = (f32[1152,16]{0,1:T(8,128)S(1)}, f32[1152,16]{0,1:T(8,128)}, u32[]{:S(2)}) copy-start(f32[1152,16]{0,1:T(8,128)} %copy-done.3) | copy-start | bytes 221188
  143.1 5.2 %copy-start.6 = (f32[1152,16]{0,1:T(8,128)S(1)}, f32[1152,16]{0,1:T(8,128)}, u32[]{:S(2)}) copy-start(f32[1152,16]{0,1:T(8,128)} %copy-done.5) | copy-start | bytes 221188
  146.5 1.8 copy-start.1
  206.4 52.0 %copy-start.2 = (bf16[6,1152,256]{1,2,0:T(8,128)(2,1)S(1)}, bf16[6,1152,256]{1,2,0:T(8,128)(2,1)}, u32[]{:S(2)}) copy-start(bf16[6,1152,256]{1,2,0:T(8,128)(2,1)} %copy-done.1) | copy-start | bytes 10616836
  206.4 52.0 %copy-start.10 = (f32[1,256]{1,0:T(1,128)S(1)}, f32[1,256]{1,0:T(1,128)}, u32[]{:S(2)}) copy-start(f32[1,256]{1,0:T(1,128)} %get-tuple-element.17) | copy-start | bytes 3076
  206.4 52.1 %copy-start.13 = (bf16[2,256,256]{2,1,0:T(8,128)(2,1)S(1)}, bf16[2,256,256]{2,1,0:T(8,128)(2,1)}, u32[]{:S(2)}) copy-start(bf16[2,256,256]{2,1,0:T(8,128)(2,1)} %param.8) | copy-start | bytes 786436
  263.3 5.8 %copy-start.14 = (bf16[20,256]{1,0:T(8,128)(2,1)S(1)}, bf16[20,256]{1,0:T(8,128)(2,1)}, u32[]{:S(2)}) copy-start(bf16[20,256]{1,0:T(8,128)(2,1)} %param.11) | copy-start | bytes 30724
where the time goes:
time: 279 us; the launch traced here: 278 us
  blocking collectives  96.5 us (35%)
  waiting for transfers between devices  76.4 us (27%)
  starting transfers between devices  41.7 us (15%)
  matrix products  32.2 us (12%)
  local copies, waits for them, and re-layouts  23.7 us (8%)
  other arithmetic  7.23 us (3%)
    all_to_all x1, blocking collectives, sent_and_summed(): lax.all_to_all(in_blocks(value, dim, peers), axis, 0, 0, tiled=True)  49.1 us
    all_to_all x1, blocking collectives, from_everyone(): lax.all_to_all(jnp.broadcast_to(value[None], (peers, *value.shape)), axis...  47.4 us
    all_to_all x1, waiting for transfers between devices, from_everyone(): lax.all_to_all(jnp.broadcast_to(value[None], (peers, *value.shape)), axis...  38.2 us
    all_to_all x1, waiting for transfers between devices, sent_and_summed(): lax.all_to_all(in_blocks(value, dim, peers), axis, 0, 0, tiled=True)  38.2 us
    all_to_all x1, starting transfers between devices, sent_and_summed(): lax.all_to_all(in_blocks(value, dim, peers), axis, 0, 0, tiled=True)  34.3 us
    dot_general x8, matrix products, product(): jnp.einsum('mi,mio->mo', vectors, matrices, preferred_element_type=jnp.fl...  9.93 us
    dot_general x2, matrix products, per_device(): jnp.dot(current.reshape(-1, channels), local_weight[layer_index], preferr...  8.31 us
    all_to_all x1, starting transfers between devices, from_everyone(): lax.all_to_all(jnp.broadcast_to(value[None], (peers, *value.shape)), axis...  7.36 us
  transfers between devices with their start and end apart: 2, of which 2 were waited for; matrix products, arithmetic and copies ran while one was open for 3% of the time, Pallas kernels for 0%

commit v1 on v0

v1 whole, which is shorter than its diff:
```python
import functools

import jax
import jax.numpy as jnp
import numpy as np
from jax import lax
from jax.experimental import pallas as pl
from jax.experimental.pallas import tpu as pltpu
from jax.sharding import PartitionSpec as P

KY = 16
KX = 16
LAYERS = 2
MODES = KY * KX
CORES = 2
BF = jnp.bfloat16
F32 = jnp.float32
MESH = pl.DeviceIdType.MESH


def zonal_tables(columns):
    phase = np.arange(columns)[:, None] * np.arange(1, KX + 1)[None, :] % columns
    angles = np.float32(2.0 * np.pi / columns) * phase.astype(np.float32)
    cosines, sines = np.cos(angles), np.sin(angles)
    forward = np.concatenate([cosines, -sines], axis=1) / np.sqrt(np.float32(columns))
    inverse = np.stack([cosines, -sines], axis=2).reshape(columns, 2 * KX)
    inverse = inverse * np.sqrt(np.float32(2.0 / KX))
    return forward.T.astype(BF), inverse.astype(BF)


def meridional_tables(devices, rows_here):
    height = devices * rows_here
    index = np.arange(KY)
    waves = np.where(index < KY // 2, index, index - KY)
    rows = np.arange(rows_here)[None, :] * devices + np.arange(devices)[:, None]
    phase = waves[None, :, None] * rows[:, None, :] % height
    angles = np.float32(2.0 * np.pi / height) * phase.astype(np.float32)
    cosines, sines = np.cos(angles), np.sin(angles)
    forward = np.stack([np.stack([cosines, sines], -1), np.stack([-sines, cosines], -1)], 2)
    forward = forward / np.sqrt(np.float32(height))
    cos_t, sin_t = cosines.transpose(0, 2, 1), sines.transpose(0, 2, 1)
    inverse = np.stack([np.stack([cos_t, -sin_t], -1), np.stack([sin_t, cos_t], -1)], 2)
    inverse = inverse / np.sqrt(np.float32(KY))
    pairs = 2 * rows_here
    padded_f = np.zeros((devices, 2 * KY, 128), np.float32)
    padded_f[:, :, :pairs] = forward.reshape(devices, 2 * KY, pairs)
    padded_i = np.zeros((devices, -(-pairs // 16) * 16, 128), np.float32)
    padded_i[:, :pairs, : 2 * KY] = inverse.reshape(devices, pairs, 2 * KY)
    return padded_f.astype(BF), padded_i.astype(BF)


def selection_tables(devices, rows_here):
    each = MODES // devices
    chips = devices // CORES
    core, chip, one, part = np.meshgrid(
        np.arange(CORES), np.arange(chips), np.arange(each), np.arange(2), indexing="ij"
    )
    mode = ((chip * CORES + core) * each + one).reshape(-1)
    part = part.reshape(-1)
    wave_y, wave_x = mode // KX, mode % KX
    pick_mode = (wave_y * 2 + part)[:, None] == np.arange(128)[None, :]
    h, r, k = np.meshgrid(np.arange(rows_here), np.arange(2), np.arange(KX), indexing="ij")
    pick_in = np.arange(128)[:, None] == (h * 2 + r).reshape(-1)[None, :]
    mask_in = wave_x[:, None] == k.reshape(-1)[None, :]
    h, k, p = np.meshgrid(np.arange(rows_here), np.arange(KX), np.arange(2), indexing="ij")
    pairs = -(-2 * rows_here // 16) * 16
    pick_out = (h * 2 + p).reshape(-1)[:, None] == np.arange(pairs)[None, :]
    mask_out = k.reshape(-1)[:, None] == wave_x[None, :]
    tables = (pick_mode[:, : 2 * KY], pick_in, mask_in, pick_out, pick_mode.T, mask_out)
    return tuple(np.asarray(t, np.float32).astype(BF) for t in tables)


def dot(a, b):
    return jnp.dot(a, b, preferred_element_type=F32)


def gelu(v):
    half = 0.5 * v
    scale = float(np.sqrt(2.0 / np.pi))
    return half + half * jnp.tanh(v * (scale + (scale * 0.044715) * (v * v)))


def kernel(
    x_hbm, sw_hbm, lw_hbm, bias_hbm, rh_hbm, rf_hbm, zf_hbm, zi_hbm, tf_hbm, ti_hbm,
    pm_hbm, pin_hbm, min_hbm, pout_hbm, pmt_hbm, mout_hbm,
    out_ref,
    state, sw, lw, bias, rh, rf, zf, zi, tf, ti, pm, pin, minn, pout, pmt, mout,
    m2, n2, zonal, pw, returned, xsend, xrecv, pbuf, rbuf, mall,
    in_sem, sw_sem, small_sem, late_sem,
    xs_sem, xr_sem, rs_send, rs_recv, ag_send, ag_recv, d2_send, d2_recv,
):
    rows_here, columns, channels = state.shape
    devices = lax.axis_size("space")
    chips = devices // CORES
    me = lax.axis_index("space")
    core = lax.rem(me, CORES)
    chip = me // CORES
    other = 1 - core
    partner = chip * CORES + other
    half = chips // 2
    step = 384 if columns % 384 == 0 else columns
    tiles = [(t * step, step) for t in range(columns // step)]

    def peer(distance):
        return lax.rem(chip + distance, chips) * CORES + core

    barrier = pltpu.get_barrier_semaphore()

    def greet(distance, carry):
        pl.semaphore_signal(barrier, inc=1, device_id={"space": peer(distance)}, device_id_type=MESH)
        return carry

    pl.semaphore_signal(barrier, inc=1, device_id={"space": partner}, device_id_type=MESH)
    lax.fori_loop(1, chips, greet, 0)

    small = [
        (zf_hbm, zf), (tf_hbm.at[me], tf), (pm_hbm, pm), (pin_hbm, pin), (min_hbm, minn),
    ]
    late = [
        (lw_hbm, lw), (bias_hbm, bias), (zi_hbm, zi), (ti_hbm.at[me], ti), (pout_hbm, pout),
        (pmt_hbm, pmt), (mout_hbm, mout), (rh_hbm, rh), (rf_hbm, rf),
    ]
    small_copies = [pltpu.make_async_copy(a, b, small_sem.at[i]) for i, (a, b) in enumerate(small)]
    late_copies = [pltpu.make_async_copy(a, b, late_sem.at[i]) for i, (a, b) in enumerate(late)]
    in_copies = [
        pltpu.make_async_copy(x_hbm.at[h], state.at[h], in_sem.at[h]) for h in range(rows_here)
    ]
    sw_copies = [pltpu.make_async_copy(sw_hbm.at[l], sw.at[l], sw_sem.at[l]) for l in range(LAYERS)]
    for copy in small_copies + in_copies + late_copies + sw_copies:
        copy.start()

    for copy in small_copies:
        copy.wait()
    spread_f = dot(dot(pm[...], tf[...]).astype(BF), pin[...]) * minn[...].astype(F32)
    m2[...] = spread_f.astype(BF).reshape(m2.shape)

    for h in range(rows_here):
        in_copies[h].wait()
        zonal[pl.ds(h * 2 * KX, 2 * KX), :] = dot(zf[...], state[h]).astype(BF)

    def send_partials_to_partner(layer):
        xsend[layer] = dot(m2[other], zonal[...]).astype(BF)
        copy = pltpu.make_async_remote_copy(
            src_ref=xsend.at[layer], dst_ref=xrecv.at[layer], send_sem=xs_sem.at[layer],
            recv_sem=xr_sem.at[layer], device_id={"space": partner}, device_id_type=MESH,
        )
        copy.start()
        return copy

    def reduce_sends(layer, partner_copy):
        mine = dot(m2[core], zonal[...])
        partner_copy.wait()
        mine = mine + xrecv[layer].astype(F32)
        pbuf[layer] = mine.reshape(pbuf.shape[1:]).astype(BF)

        def send(distance):
            pltpu.make_async_remote_copy(
                src_ref=pbuf.at[layer, lax.rem(chip + distance, chips)],
                dst_ref=rbuf.at[layer, distance], send_sem=rs_send.at[layer],
                recv_sem=rs_recv.at[layer], device_id={"space": peer(distance)},
                device_id_type=MESH,
            ).start()

        send(half)

        def body(i, carry):
            send(half - 1 - i)
            send(half + 1 + i)
            return carry

        lax.fori_loop(0, half - 1, body, 0)

    def wait_bytes(ref, sem):
        pltpu.make_async_copy(ref, ref, sem).wait()

    def pointwise(layer):
        row_bias = bias[pl.ds(layer, 1), :].astype(F32)

        def body(h, carry):
            for start, size in tiles:
                value = dot(state[h, pl.ds(start, size), :], lw[layer]) + row_bias
                pw[h, pl.ds(start, size), :] = value
            return carry

        lax.fori_loop(0, rows_here, body, 0)

    def reduce_finish_and_mix(layer):
        wait_bytes(rbuf.at[layer, pl.ds(1, chips - 1)], rs_recv.at[layer])
        total = pbuf[layer, chip].astype(F32)
        total = total + jnp.sum(rbuf[layer, pl.ds(1, chips - 1)].astype(F32), axis=0)
        spectrum = total.astype(BF).astype(F32)
        count = spectrum.shape[0]
        row = lax.broadcasted_iota(jnp.int32, spectrum.shape, 0)
        turned = jnp.where(
            row % 2 == 0, -pltpu.roll(spectrum, count - 1, 0), pltpu.roll(spectrum, 1, 0)
        )
        pieces = []
        for mode in range(count // 2):
            here = row // 2 == mode
            pieces.append(jnp.where(here, spectrum, 0.0))
            pieces.append(jnp.where(here, turned, 0.0))
        left = jnp.concatenate(pieces, axis=1).astype(BF)
        mixed = dot(left, sw[layer].reshape(-1, channels))
        mall[layer, core, chip] = mixed.astype(BF)

    def gather(layer):
        own = mall.at[layer, core, chip]

        def send(distance):
            pltpu.make_async_remote_copy(
                src_ref=own, dst_ref=own, send_sem=ag_send.at[layer],
                recv_sem=ag_recv.at[layer, distance], device_id={"space": peer(distance)},
                device_id_type=MESH,
            ).start()

        def relay(source):
            piece = mall.at[layer, core, source]
            pltpu.make_async_remote_copy(
                src_ref=piece, dst_ref=piece, send_sem=d2_send.at[layer],
                recv_sem=d2_recv.at[layer], device_id={"space": partner}, device_id_type=MESH,
            ).start()

        def pass_on(distance):
            source = lax.rem(chip + chips - distance, chips)
            wait_bytes(mall.at[layer, core, source], ag_recv.at[layer, distance])
            relay(source)

        send(half)

        def send_body(i, carry):
            send(half - 1 - i)
            send(half + 1 + i)
            return carry

        lax.fori_loop(0, half - 1, send_body, 0)
        relay(chip)

        def relay_body(i, carry):
            pass_on(1 + i)
            pass_on(chips - 1 - i)
            return carry

        lax.fori_loop(0, half - 1, relay_body, 0)
        pass_on(half)
        wait_bytes(mall.at[layer, other], d2_recv.at[layer])
        modes = mall[layer].astype(F32).reshape(2 * MODES, channels).astype(BF)
        returned[...] = dot(n2[...], modes).astype(BF)

    for copy in late_copies:
        copy.wait()
    spread_i = dot(dot(pout[...], ti[...]).astype(BF), pmt[...]) * mout[...].astype(F32)
    n2[...] = spread_i.astype(BF)
    pointwise(0)
    for copy in sw_copies:
        copy.wait()
    pl.semaphore_wait(barrier, chips)

    reduce_sends(0, send_partials_to_partner(0))
    reduce_finish_and_mix(0)
    gather(0)

    def finish_body(h, carry):
        back = returned[pl.ds(pl.multiple_of(h * 2 * KX, 2 * KX), 2 * KX), :]
        part = jnp.zeros((2 * KX, channels), F32)
        for start, size in tiles:
            value = dot(zi[pl.ds(start, size), :], back) + pw[h, pl.ds(start, size), :]
            value = gelu(value).astype(BF)
            state[h, pl.ds(start, size), :] = value
            part = part + dot(zf[:, pl.ds(start, size)], value)
        zonal[pl.ds(pl.multiple_of(h * 2 * KX, 2 * KX), 2 * KX), :] = part.astype(BF)
        return carry

    lax.fori_loop(0, rows_here, finish_body, 0)

    reduce_sends(1, send_partials_to_partner(1))
    pointwise(1)
    reduce_finish_and_mix(1)
    gather(1)

    def readout_body(h, carry):
        back = returned[pl.ds(pl.multiple_of(h * 2 * KX, 2 * KX), 2 * KX), :]
        for start, size in tiles:
            value = dot(zi[pl.ds(start, size), :], back) + pw[h, pl.ds(start, size), :]
            value = gelu(value).astype(BF)
            hidden = gelu(dot(value, rh[...])).astype(BF)
            final = lax.dot_general(
                rf[...], hidden, (((1,), (1,)), ((), ())), preferred_element_type=F32
            )
            out_ref[h, :, pl.ds(start, size)] = final.astype(BF)
        return carry

    lax.fori_loop(0, rows_here, readout_body, 0)

    for layer in range(LAYERS):
        wait_bytes(pbuf.at[layer, pl.ds(1, chips - 1)], rs_send.at[layer])
        wait_bytes(rbuf.at[layer, pl.ds(1, chips - 1)], ag_send.at[layer])
        wait_bytes(mall.at[layer, core], d2_send.at[layer])


def per_device(inputs, spectral_weight, local_weight, layer_bias, readout_hidden, readout_final):
    rows_here, columns, channels = inputs.shape
    devices = lax.axis_size("space")
    chips = devices // CORES
    each = MODES // devices
    variables, units = readout_final.shape
    zonal_forward, zonal_inverse = zonal_tables(columns)
    table_f, table_i = meridional_tables(devices, rows_here)
    selections = selection_tables(devices, rows_here)
    bands = rows_here * 2 * KX
    operands = (
        inputs, spectral_weight, local_weight, layer_bias, readout_hidden, readout_final,
        zonal_forward, zonal_inverse, table_f, table_i, *selections,
    )
    vmem = pltpu.VMEM
    like = lambda a, cut=0: vmem(a.shape[cut:], BF)
    result = pl.pallas_call(
        kernel,
        name="operator",
        out_shape=jax.ShapeDtypeStruct((rows_here, variables, columns), BF),
        in_specs=[pl.BlockSpec(memory_space=pltpu.HBM)] * len(operands),
        out_specs=pl.BlockSpec(memory_space=pltpu.VMEM),
        scratch_shapes=[
            *[like(a) for a in operands[:8]],
            like(table_f, 1),
            like(table_i, 1),
            *[like(a) for a in selections],
            vmem((CORES, MODES, bands), BF),
            vmem((bands, 2 * MODES), BF),
            vmem((bands, channels), BF),
            vmem((rows_here, columns, channels), F32),
            vmem((bands, channels), BF),
            vmem((LAYERS, MODES, channels), BF),
            vmem((LAYERS, MODES, channels), BF),
            vmem((LAYERS, chips, 2 * each, channels), BF),
            vmem((LAYERS, chips, 2 * each, channels), BF),
            vmem((LAYERS, CORES, chips, 2 * each, channels), BF),
            pltpu.SemaphoreType.DMA((rows_here,)),
            pltpu.SemaphoreType.DMA((LAYERS,)),
            pltpu.SemaphoreType.DMA((5,)),
            pltpu.SemaphoreType.DMA((9,)),
            pltpu.SemaphoreType.DMA((LAYERS,)),
            pltpu.SemaphoreType.DMA((LAYERS,)),
            pltpu.SemaphoreType.DMA((LAYERS,)),
            pltpu.SemaphoreType.DMA((LAYERS,)),
            pltpu.SemaphoreType.DMA((LAYERS,)),
            pltpu.SemaphoreType.DMA((LAYERS, chips)),
            pltpu.SemaphoreType.DMA((LAYERS,)),
            pltpu.SemaphoreType.DMA((LAYERS,)),
        ],
        compiler_params=pltpu.CompilerParams(
            collective_id=0, has_side_effects=True, vmem_limit_bytes=60 * 1024 * 1024
        ),
    )(*operands)
    return jnp.transpose(result, (1, 0, 2))


def solution(mesh):
    in_specs = (
        P(("groups", "space"), None, None),
        P(None, "space", None, None, None),
        P(),
        P(),
        P(),
        P(),
    )
    out_specs = P(None, ("groups", "space"), None)
    return jax.shard_map(
        per_device, mesh=mesh, in_specs=in_specs, out_specs=out_specs, check_vma=False
    )
```

time: 279 us -> 117 us (0.42)
  Pallas kernels: 0 us -> 115 us
  blocking collectives: 96.5 us -> 0 us
  waiting for transfers between devices: 76.4 us -> 0 us
  starting transfers between devices: 41.7 us -> 0 us
  matrix products: 32.2 us -> 0 us
  local copies, waits for them, and re-layouts: 23.7 us -> 1.73 us
  other arithmetic: 7.23 us -> 0 us
    pallas_call x0 -> x1, Pallas kernels: none -> 115 us  [per_device(): pl.pallas_call(kernel, name='operator', out_shape=jax.ShapeDtypeStruct((r...]
    all_to_all x2 -> x0, blocking collectives: 96.5 us -> none  [the longest x1 49.1 us: sent_and_summed(): lax.all_to_all(in_blocks(value, dim, peers), axis, 0, 0, tiled=True)]
    all_to_all x2 -> x0, waiting for transfers between devices: 76.4 us -> none  [the longest x1 38.2 us: from_everyone(): lax.all_to_all(jnp.broadcast_to(value[None], (peers, *value.shape)), axis...]
    all_to_all x2 -> x0, starting transfers between devices: 41.7 us -> none  [the longest x1 34.3 us: sent_and_summed(): lax.all_to_all(in_blocks(value, dim, peers), axis, 0, 0, tiled=True)]
    dot_general x19 -> x0, matrix products: 32.2 us -> none  [the longest x8 9.93 us: product(): jnp.einsum('mi,mio->mo', vectors, matrices, preferred_element_type=jnp.fl...]
    convert_element_type x5 -> x0, local copies, waits for them, and re-layouts: 11.3 us -> none  [the longest x1 5.77 us: per_device(): jax.nn.gelu(spread + pointwise + bias_now, approximate=True)]
    reshape x2 -> x0, local copies, waits for them, and re-layouts: 3.82 us -> none  [per_device(): final.astype(jnp.bfloat16)]
    squeeze x3 -> x0, local copies, waits for them, and re-layouts: 3.78 us -> none  [the longest x1 3.07 us: per_device(): spectral_weight[layer_index]]
  transfers between devices with their start and end apart: 2 -> 0, of which waited for: 2 -> 0; matrix products, arithmetic and copies ran while one was open for 3% -> 0% of each run, Pallas kernels for 0% -> 0%
where the time goes in v1:
time: 117 us; the launch traced here: 116 us
  Pallas kernels  115 us (98%)
  local copies, waits for them, and re-layouts  1.73 us (1%)
    pallas_call x1, Pallas kernels, per_device(): pl.pallas_call(kernel, name='operator', out_shape=jax.ShapeDtypeStruct((r...  115 us

profile of v1, /device:TPU:37, one launch (start us, length us, event | category | flops | bytes accessed | tf_op | source)
XLA Modules:
  0.0 116.4 jit_solution(1976454224868952752)
XLA Ops:
  0.0 114.7 %operator.1 = bf16[6,20,1152]{2,1,0:T(8,128)(2,1)} custom-call(bf16[6,1152,256]{2,1,0:T(8,128)(2,1)} %x_hbm.1, bf16[2,4,2,256,256]{4,3,2,1,0:T(8,128)(2,1)} %sw_hbm.1, bf16[2,256,256]{2,1,0:T(8,128)(2,1)} %lw_hbm.1, bf16[2,256]{1,0:T(2,128)(2,1)} %bias_hbm.1, bf16[256,256]{1,0:T(8,128)(2,1)} %rh_hbm.1, bf16[20,256]{1,0:T(8,128)(2,1)} %rf_hbm.1, ...), custom_call_target="tpu_custom_call" | custom-call | tf_op jit(solution)/shard_map/operator/pallas_call | solution.py:316
  114.7 1.7 %copy.18 = bf16[20,6,1152]{2,0,1:T(8,128)(2,1)} copy(bf16[20,6,1152]{2,0,1:T(8,128)(2,1)} %bitcast.1) | data formatting | bytes 552960

commit v2 on v1

--- a/solution.py
+++ b/solution.py
@@ -80,14 +80,23 @@
     return half + half * jnp.tanh(v * (scale + (scale * 0.044715) * (v * v)))
 
 
+def routes(chips):
+    half = chips // 2
+    hubs = [h for h in (10, 5) if h + 2 < half]
+    reach = (2, -2, 1, -1)
+    covered = {h + w for h in hubs for w in (-2, -1, 0, 1, 2)}
+    direct = [half] + [s * d for d in range(half - 1, 0, -1) if d not in covered for s in (1, -1)]
+    return direct, [s * h for h in hubs for s in (1, -1)], reach
+
+
 def kernel(
     x_hbm, sw_hbm, lw_hbm, bias_hbm, rh_hbm, rf_hbm, zf_hbm, zi_hbm, tf_hbm, ti_hbm,
     pm_hbm, pin_hbm, min_hbm, pout_hbm, pmt_hbm, mout_hbm,
     out_ref,
     state, sw, lw, bias, rh, rf, zf, zi, tf, ti, pm, pin, minn, pout, pmt, mout,
-    m2, n2, zonal, pw, returned, xsend, xrecv, pbuf, rbuf, mall,
+    m2, n2, zonal, pw, returned, xsend, xrecv, pbuf, rbuf, cbuf, hbuf, mall,
     in_sem, sw_sem, small_sem, late_sem,
-    xs_sem, xr_sem, rs_send, rs_recv, ag_send, ag_recv, d2_send, d2_recv,
+    xs_sem, xr_sem, rs_send, rs_stage, rs_recv, ag_send, ag_recv, d2_send, d2_recv,
 ):
     rows_here, columns, channels = state.shape
     devices = lax.axis_size("space")
@@ -97,21 +106,24 @@
     chip = me // CORES
     other = 1 - core
     partner = chip * CORES + other
-    half = chips // 2
+    direct, hubs, reach = routes(chips)
+    far = [d for d in direct if abs(d) > max(map(abs, hubs), default=0)]
+    near = [d for d in direct if d not in far]
+    final_slot = {d: i for i, d in enumerate(direct + hubs)}
     step = 384 if columns % 384 == 0 else columns
     tiles = [(t * step, step) for t in range(columns // step)]
 
+    def chip_at(distance):
+        return lax.rem(chip + distance + chips, chips)
+
     def peer(distance):
-        return lax.rem(chip + distance, chips) * CORES + core
+        return chip_at(distance) * CORES + core
 
     barrier = pltpu.get_barrier_semaphore()
 
-    def greet(distance, carry):
-        pl.semaphore_signal(barrier, inc=1, device_id={"space": peer(distance)}, device_id_type=MESH)
-        return carry
-
-    pl.semaphore_signal(barrier, inc=1, device_id={"space": partner}, device_id_type=MESH)
-    lax.fori_loop(1, chips, greet, 0)
+    greeted = [peer(d) for d in direct + hubs] + [partner]
+    for target in greeted:
+        pl.semaphore_signal(barrier, inc=1, device_id={"space": target}, device_id_type=MESH)
 
     small = [
         (zf_hbm, zf), (tf_hbm.at[me], tf), (pm_hbm, pm), (pin_hbm, pin), (min_hbm, minn),
@@ -155,20 +167,44 @@
 
         def send(distance):
             pltpu.make_async_remote_copy(
-                src_ref=pbuf.at[layer, lax.rem(chip + distance, chips)],
-                dst_ref=rbuf.at[layer, distance], send_sem=rs_send.at[layer],
+                src_ref=pbuf.at[layer, chip_at(distance)],
+                dst_ref=rbuf.at[layer, final_slot[distance]], send_sem=rs_send.at[layer],
                 recv_sem=rs_recv.at[layer], device_id={"space": peer(distance)},
                 device_id_type=MESH,
             ).start()
 
-        send(half)
-
-        def body(i, carry):
-            send(half - 1 - i)
-            send(half + 1 + i)
-            return carry
-
-        lax.fori_loop(0, half - 1, body, 0)
+        def stage(hub):
+            index = hubs.index(hub)
+            for slot, offset in enumerate(reach):
+                pltpu.make_async_remote_copy(
+                    src_ref=pbuf.at[layer, chip_at(offset + hub)],
+                    dst_ref=cbuf.at[layer, index, slot], send_sem=rs_send.at[layer],
+                    recv_sem=rs_stage.at[layer, index], device_id={"space": peer(offset)},
+                    device_id_type=MESH,
+                ).start()
+
+        for distance in far[:3]:
+            send(distance)
+        for hub in hubs[:2]:
+            stage(hub)
+        for distance in far[3:]:
+            send(distance)
+        for hub in hubs[2:]:
+            stage(hub)
+        for distance in near:
+            send(distance)
+
+    def reduce_hubs(layer):
+        for index, hub in enumerate(hubs):
+            wait_bytes(cbuf.at[layer, index], rs_stage.at[layer, index])
+            total = pbuf[layer, chip_at(hub)].astype(F32)
+            total = total + jnp.sum(cbuf[layer, index].astype(F32), axis=0)
+            hbuf[layer, index] = total.astype(BF)
+            pltpu.make_async_remote_copy(
+                src_ref=hbuf.at[layer, index], dst_ref=rbuf.at[layer, final_slot[hub]],
+                send_sem=rs_send.at[layer], recv_sem=rs_recv.at[layer],
+                device_id={"space": peer(hub)}, device_id_type=MESH,
+            ).start()
 
     def wait_bytes(ref, sem):
         pltpu.make_async_copy(ref, ref, sem).wait()
@@ -185,9 +221,9 @@
         lax.fori_loop(0, rows_here, body, 0)
 
     def reduce_finish_and_mix(layer):
-        wait_bytes(rbuf.at[layer, pl.ds(1, chips - 1)], rs_recv.at[layer])
+        wait_bytes(rbuf.at[layer], rs_recv.at[layer])
         total = pbuf[layer, chip].astype(F32)
-        total = total + jnp.sum(rbuf[layer, pl.ds(1, chips - 1)].astype(F32), axis=0)
+        total = total + jnp.sum(rbuf[layer].astype(F32), axis=0)
         spectrum = total.astype(BF).astype(F32)
         count = spectrum.shape[0]
         row = lax.broadcasted_iota(jnp.int32, spectrum.shape, 0)
@@ -206,42 +242,45 @@
     def gather(layer):
         own = mall.at[layer, core, chip]
 
-        def send(distance):
+        def send(piece, target, distance):
             pltpu.make_async_remote_copy(
-                src_ref=own, dst_ref=own, send_sem=ag_send.at[layer],
-                recv_sem=ag_recv.at[layer, distance], device_id={"space": peer(distance)},
-                device_id_type=MESH,
+                src_ref=piece, dst_ref=piece, send_sem=ag_send.at[layer],
+                recv_sem=ag_recv.at[layer, distance % chips],
+                device_id={"space": peer(target)}, device_id_type=MESH,
             ).start()
 
-        def relay(source):
-            piece = mall.at[layer, core, source]
+        def relay(piece):
             pltpu.make_async_remote_copy(
                 src_ref=piece, dst_ref=piece, send_sem=d2_send.at[layer],
                 recv_sem=d2_recv.at[layer], device_id={"space": partner}, device_id_type=MESH,
             ).start()
 
-        def pass_on(distance):
-            source = lax.rem(chip + chips - distance, chips)
-            wait_bytes(mall.at[layer, core, source], ag_recv.at[layer, distance])
-            relay(source)
-
-        send(half)
-
-        def send_body(i, carry):
-            send(half - 1 - i)
-            send(half + 1 + i)
-            return carry
-
-        lax.fori_loop(0, half - 1, send_body, 0)
-        relay(chip)
-
-        def relay_body(i, carry):
-            pass_on(1 + i)
-            pass_on(chips - 1 - i)
-            return carry
-
-        lax.fori_loop(0, half - 1, relay_body, 0)
-        pass_on(half)
+        def arrived(distance):
+            piece = mall.at[layer, core, chip_at(-distance)]
+            wait_bytes(piece, ag_recv.at[layer, distance % chips])
+            return piece
+
+        for distance in far[:3] + hubs[:2] + far[3:] + hubs[2:] + near:
+            send(own, distance, distance)
+        relay(own)
+        for distance in reversed(near):
+            relay(arrived(distance))
+        for hub in hubs[2:] + hubs[:2]:
+            piece = arrived(hub)
+            for offset in reach:
+                send(piece, offset, hub + offset)
+            relay(piece)
+        behind = far[:0:-1]
+        for hub in hubs[2:]:
+            for offset in reach:
+                relay(arrived(hub + offset))
+        for distance in behind[:4]:
+            relay(arrived(distance))
+        for hub in hubs[:2]:
+            for offset in reach:
+                relay(arrived(hub + offset))
+        for distance in behind[4:] + far[:1]:
+            relay(arrived(distance))
         wait_bytes(mall.at[layer, other], d2_recv.at[layer])
         modes = mall[layer].astype(F32).reshape(2 * MODES, channels).astype(BF)
         returned[...] = dot(n2[...], modes).astype(BF)
@@ -250,12 +289,13 @@
         copy.wait()
     spread_i = dot(dot(pout[...], ti[...]).astype(BF), pmt[...]) * mout[...].astype(F32)
     n2[...] = spread_i.astype(BF)
-    pointwise(0)
     for copy in sw_copies:
         copy.wait()
-    pl.semaphore_wait(barrier, chips)
+    pl.semaphore_wait(barrier, len(greeted))
 
     reduce_sends(0, send_partials_to_partner(0))
+    pointwise(0)
+    reduce_hubs(0)
     reduce_finish_and_mix(0)
     gather(0)
 
@@ -274,6 +314,7 @@
 
     reduce_sends(1, send_partials_to_partner(1))
     pointwise(1)
+    reduce_hubs(1)
     reduce_finish_and_mix(1)
     gather(1)
 
@@ -293,7 +334,7 @@
 
     for layer in range(LAYERS):
         wait_bytes(pbuf.at[layer, pl.ds(1, chips - 1)], rs_send.at[layer])
-        wait_bytes(rbuf.at[layer, pl.ds(1, chips - 1)], ag_send.at[layer])
+        wait_bytes(pbuf.at[layer, pl.ds(1, chips - 1)], ag_send.at[layer])
         wait_bytes(mall.at[layer, core], d2_send.at[layer])
 
 
@@ -302,6 +343,7 @@
     devices = lax.axis_size("space")
     chips = devices // CORES
     each = MODES // devices
+    direct, hubs, reach = routes(chips)
     variables, units = readout_final.shape
     zonal_forward, zonal_inverse = zonal_tables(columns)
     table_f, table_i = meridional_tables(devices, rows_here)
@@ -332,7 +374,9 @@
             vmem((LAYERS, MODES, channels), BF),
             vmem((LAYERS, MODES, channels), BF),
             vmem((LAYERS, chips, 2 * each, channels), BF),
-            vmem((LAYERS, chips, 2 * each, channels), BF),
+            vmem((LAYERS, len(direct) + len(hubs), 2 * each, channels), BF),
+            vmem((LAYERS, len(hubs), len(reach), 2 * each, channels), BF),
+            vmem((LAYERS, len(hubs), 2 * each, channels), BF),
             vmem((LAYERS, CORES, chips, 2 * each, channels), BF),
             pltpu.SemaphoreType.DMA((rows_here,)),
             pltpu.SemaphoreType.DMA((LAYERS,)),
@@ -341,6 +385,7 @@
             pltpu.SemaphoreType.DMA((LAYERS,)),
             pltpu.SemaphoreType.DMA((LAYERS,)),
             pltpu.SemaphoreType.DMA((LAYERS,)),
+            pltpu.SemaphoreType.DMA((LAYERS, len(hubs))),
             pltpu.SemaphoreType.DMA((LAYERS,)),
             pltpu.SemaphoreType.DMA((LAYERS,)),
             pltpu.SemaphoreType.DMA((LAYERS, chips)),
@@ -348,9 +393,9 @@
             pltpu.SemaphoreType.DMA((LAYERS,)),
         ],
         compiler_params=pltpu.CompilerParams(
-            collective_id=0, has_side_effects=True, vmem_limit_bytes=60 * 1024 * 1024
+            collective_id=0, has_side_effects=True, vmem_limit_bytes=50 * 1024 * 1024
         ),
-    )(*operands)
+    )(*[pltpu.with_memory_space_constraint(jnp.asarray(a), pltpu.HBM) for a in operands])
     return jnp.transpose(result, (1, 0, 2))
 
 

time: 117 us -> 108 us (0.923)
  Pallas kernels: 115 us -> 107 us
    pallas_call x1, Pallas kernels: 115 us -> 107 us  [per_device(): pl.pallas_call(kernel, name='operator', out_shape=jax.ShapeDtypeStruct((r...]
where the time goes in v2:
time: 108 us
  Pallas kernels  107 us (99%)
    pallas_call x1, Pallas kernels, per_device(): pl.pallas_call(kernel, name='operator', out_shape=jax.ShapeDtypeStruct((r...  107 us

profile of v2, /device:TPU:37, one launch (start us, length us, event | category | flops | bytes accessed | tf_op | source)
XLA Modules:
  0.0 107.8 jit_solution(9582021396348097217)
XLA Ops:
  0.0 107.1 %operator.1 = bf16[6,20,1152]{2,1,0:T(8,128)(2,1)S(1)} custom-call(bf16[6,1152,256]{2,1,0:T(8,128)(2,1)} %x_hbm.1, bf16[2,4,2,256,256]{4,3,2,1,0:T(8,128)(2,1)} %sw_hbm.1, bf16[2,256,256]{2,1,0:T(8,128)(2,1)} %lw_hbm.1, bf16[2,256]{1,0:T(2,128)(2,1)} %bias_hbm.1, bf16[256,256]{1,0:T(8,128)(2,1)} %rh_hbm.1, bf16[20,256]{1,0:T(8,128)(2,1)} %rf_hbm.1, ...), custom_call_target="tpu_custom_call" | custom-call | tf_op jit(solution)/shard_map/operator/pallas_call | solution.py:358
  107.1 0.7 copy.18

commit v3 on v2

--- a/solution.py
+++ b/solution.py
@@ -25,7 +25,7 @@
     forward = np.concatenate([cosines, -sines], axis=1) / np.sqrt(np.float32(columns))
     inverse = np.stack([cosines, -sines], axis=2).reshape(columns, 2 * KX)
     inverse = inverse * np.sqrt(np.float32(2.0 / KX))
-    return forward.T.astype(BF), inverse.astype(BF)
+    return forward.T.astype(BF), (0.5 * inverse).astype(BF)
 
 
 def meridional_tables(devices, rows_here):
@@ -74,19 +74,39 @@
     return jnp.dot(a, b, preferred_element_type=F32)
 
 
-def gelu(v):
-    half = 0.5 * v
+def gelu_of_half(h):
+    h = h.astype(BF)
     scale = float(np.sqrt(2.0 / np.pi))
-    return half + half * jnp.tanh(v * (scale + (scale * 0.044715) * (v * v)))
+    return h + h * jnp.tanh(h * (2.0 * scale + (8.0 * scale * 0.044715) * (h * h)))
 
 
 def routes(chips):
     half = chips // 2
-    hubs = [h for h in (10, 5) if h + 2 < half]
     reach = (2, -2, 1, -1)
-    covered = {h + w for h in hubs for w in (-2, -1, 0, 1, 2)}
+    hubs = [(s * h, reach) for h in (10, 5) for s in (1, -1) if h + 2 < half]
+    covered = {h + w for h, _ in hubs for w in (-2, -1, 0, 1, 2)}
     direct = [half] + [s * d for d in range(half - 1, 0, -1) if d not in covered for s in (1, -1)]
-    return direct, [s * h for h in hubs for s in (1, -1)], reach
+    return direct, hubs
+
+
+def short_routes(chips):
+    half = chips // 2
+    quarter = half // 2
+    start = quarter // 2
+    ahead = [d - quarter for d in range(half, start - 1, -1) if d != quarter]
+    behind = [quarter - d for d in range(half - 1, start - 1, -1) if d != quarter]
+    direct = [s * d for d in range(start - 1, 0, -1) for s in (1, -1)]
+    return direct, [(quarter, tuple(ahead)), (-quarter, tuple(behind))]
+
+
+def sending_order(direct, hubs):
+    staged = [(i, j) for j in range(max(len(w) for _, w in hubs)) for i, (_, w) in enumerate(hubs) if j < len(w)]
+    outer = max(abs(h) for h, _ in hubs)
+    far = [(d,) for d in direct if abs(d) > outer]
+    near = [(d,) for d in direct if abs(d) <= outer]
+    first = [s for s in staged if abs(hubs[s[0]][0]) == outer]
+    rest = [s for s in staged if s not in first]
+    return far[:3] + first + far[3:] + rest + near
 
 
 def kernel(
@@ -94,7 +114,7 @@
     pm_hbm, pin_hbm, min_hbm, pout_hbm, pmt_hbm, mout_hbm,
     out_ref,
     state, sw, lw, bias, rh, rf, zf, zi, tf, ti, pm, pin, minn, pout, pmt, mout,
-    m2, n2, zonal, pw, returned, xsend, xrecv, pbuf, rbuf, cbuf, hbuf, mall,
+    m2, n2, zonal, pw, returned, xsend, xrecv, pbuf, rbuf_0, cbuf_0, hbuf_0, rbuf_1, cbuf_1, hbuf_1, mall,
     in_sem, sw_sem, small_sem, late_sem,
     xs_sem, xr_sem, rs_send, rs_stage, rs_recv, ag_send, ag_recv, d2_send, d2_recv,
 ):
@@ -106,10 +126,13 @@
     chip = me // CORES
     other = 1 - core
     partner = chip * CORES + other
-    direct, hubs, reach = routes(chips)
-    far = [d for d in direct if abs(d) > max(map(abs, hubs), default=0)]
+    plans = (short_routes(chips), routes(chips))
+    landing = ((rbuf_0, cbuf_0, hbuf_0), (rbuf_1, cbuf_1, hbuf_1))
+    direct, hub_windows = plans[1]
+    hubs = [h for h, _ in hub_windows]
+    reach = hub_windows[0][1]
+    far = [d for d in direct if abs(d) > max(map(abs, hubs))]
     near = [d for d in direct if d not in far]
-    final_slot = {d: i for i, d in enumerate(direct + hubs)}
     step = 384 if columns % 384 == 0 else columns
     tiles = [(t * step, step) for t in range(columns // step)]
 
@@ -121,7 +144,8 @@
 
     barrier = pltpu.get_barrier_semaphore()
 
-    greeted = [peer(d) for d in direct + hubs] + [partner]
+    closest = max(abs(d) for hub, window in plans[0][1] for d in (hub, *window))
+    greeted = [peer(s * d) for d in range(1, closest + 1) for s in (1, -1)] + [partner]
     for target in greeted:
         pl.semaphore_signal(barrier, inc=1, device_id={"space": target}, device_id_type=MESH)
 
@@ -165,43 +189,33 @@
         mine = mine + xrecv[layer].astype(F32)
         pbuf[layer] = mine.reshape(pbuf.shape[1:]).astype(BF)
 
-        def send(distance):
+        whole, staged = plans[layer]
+        rbuf, cbuf, _ = landing[layer]
+        for step in sending_order(whole, staged):
+            if len(step) == 1:
+                source, target = chip_at(step[0]), step[0]
+                place, semaphore = rbuf.at[whole.index(step[0])], rs_recv.at[layer]
+            else:
+                index, slot = step
+                hub, window = staged[index]
+                source, target = chip_at(window[slot] + hub), window[slot]
+                place, semaphore = cbuf.at[index, slot], rs_stage.at[layer, index]
             pltpu.make_async_remote_copy(
-                src_ref=pbuf.at[layer, chip_at(distance)],
-                dst_ref=rbuf.at[layer, final_slot[distance]], send_sem=rs_send.at[layer],
-                recv_sem=rs_recv.at[layer], device_id={"space": peer(distance)},
-                device_id_type=MESH,
+                src_ref=pbuf.at[layer, source], dst_ref=place, send_sem=rs_send.at[layer],
+                recv_sem=semaphore, device_id={"space": peer(target)}, device_id_type=MESH,
             ).start()
 
-        def stage(hub):
-            index = hubs.index(hub)
-            for slot, offset in enumerate(reach):
-                pltpu.make_async_remote_copy(
-                    src_ref=pbuf.at[layer, chip_at(offset + hub)],
-                    dst_ref=cbuf.at[layer, index, slot], send_sem=rs_send.at[layer],
-                    recv_sem=rs_stage.at[layer, index], device_id={"space": peer(offset)},
-                    device_id_type=MESH,
-                ).start()
-
-        for distance in far[:3]:
-            send(distance)
-        for hub in hubs[:2]:
-            stage(hub)
-        for distance in far[3:]:
-            send(distance)
-        for hub in hubs[2:]:
-            stage(hub)
-        for distance in near:
-            send(distance)
-
     def reduce_hubs(layer):
-        for index, hub in enumerate(hubs):
-            wait_bytes(cbuf.at[layer, index], rs_stage.at[layer, index])
+        whole, staged = plans[layer]
+        rbuf, cbuf, hbuf = landing[layer]
+        for index, (hub, window) in enumerate(staged):
+            pieces = cbuf.at[index, pl.ds(0, len(window))]
+            wait_bytes(pieces, rs_stage.at[layer, index])
             total = pbuf[layer, chip_at(hub)].astype(F32)
-            total = total + jnp.sum(cbuf[layer, index].astype(F32), axis=0)
-            hbuf[layer, index] = total.astype(BF)
+            total = total + jnp.sum(pieces[...].astype(F32), axis=0)
+            hbuf[index] = total.astype(BF)
             pltpu.make_async_remote_copy(
-                src_ref=hbuf.at[layer, index], dst_ref=rbuf.at[layer, final_slot[hub]],
+                src_ref=hbuf.at[index], dst_ref=rbuf.at[len(whole) + index],
                 send_sem=rs_send.at[layer], recv_sem=rs_recv.at[layer],
                 device_id={"space": peer(hub)}, device_id_type=MESH,
             ).start()
@@ -210,20 +224,22 @@
         pltpu.make_async_copy(ref, ref, sem).wait()
 
     def pointwise(layer):
-        row_bias = bias[pl.ds(layer, 1), :].astype(F32)
+        row_bias = 0.5 * bias[pl.ds(layer, 1), :].astype(F32)
+        half_lw = lw[layer] * 0.5
 
         def body(h, carry):
             for start, size in tiles:
-                value = dot(state[h, pl.ds(start, size), :], lw[layer]) + row_bias
+                value = dot(state[h, pl.ds(start, size), :], half_lw) + row_bias
                 pw[h, pl.ds(start, size), :] = value
             return carry
 
         lax.fori_loop(0, rows_here, body, 0)
 
     def reduce_finish_and_mix(layer):
-        wait_bytes(rbuf.at[layer], rs_recv.at[layer])
+        rbuf = landing[layer][0]
+        wait_bytes(rbuf, rs_recv.at[layer])
         total = pbuf[layer, chip].astype(F32)
-        total = total + jnp.sum(rbuf[layer].astype(F32), axis=0)
+        total = total + jnp.sum(rbuf[...].astype(F32), axis=0)
         spectrum = total.astype(BF).astype(F32)
         count = spectrum.shape[0]
         row = lax.broadcasted_iota(jnp.int32, spectrum.shape, 0)
@@ -304,7 +320,7 @@
         part = jnp.zeros((2 * KX, channels), F32)
         for start, size in tiles:
             value = dot(zi[pl.ds(start, size), :], back) + pw[h, pl.ds(start, size), :]
-            value = gelu(value).astype(BF)
+            value = gelu_of_half(value)
             state[h, pl.ds(start, size), :] = value
             part = part + dot(zf[:, pl.ds(start, size)], value)
         zonal[pl.ds(pl.multiple_of(h * 2 * KX, 2 * KX), 2 * KX), :] = part.astype(BF)
@@ -318,12 +334,14 @@
     reduce_finish_and_mix(1)
     gather(1)
 
+    half_rh = rh[...] * 0.5
+
     def readout_body(h, carry):
         back = returned[pl.ds(pl.multiple_of(h * 2 * KX, 2 * KX), 2 * KX), :]
         for start, size in tiles:
             value = dot(zi[pl.ds(start, size), :], back) + pw[h, pl.ds(start, size), :]
-            value = gelu(value).astype(BF)
-            hidden = gelu(dot(value, rh[...])).astype(BF)
+            value = gelu_of_half(value)
+            hidden = gelu_of_half(dot(value, half_rh))
             final = lax.dot_general(
                 rf[...], hidden, (((1,), (1,)), ((), ())), preferred_element_type=F32
             )
@@ -343,7 +361,10 @@
     devices = lax.axis_size("space")
     chips = devices // CORES
     each = MODES // devices
-    direct, hubs, reach = routes(chips)
+    landings = []
+    for direct, hubs in (short_routes(chips), routes(chips)):
+        widest = max(len(window) for _, window in hubs)
+        landings += [(len(direct) + len(hubs),), (len(hubs), widest), (len(hubs),)]
     variables, units = readout_final.shape
     zonal_forward, zonal_inverse = zonal_tables(columns)
     table_f, table_i = meridional_tables(devices, rows_here)
@@ -374,9 +395,7 @@
             vmem((LAYERS, MODES, channels), BF),
             vmem((LAYERS, MODES, channels), BF),
             vmem((LAYERS, chips, 2 * each, channels), BF),
-            vmem((LAYERS, len(direct) + len(hubs), 2 * each, channels), BF),
-            vmem((LAYERS, len(hubs), len(reach), 2 * each, channels), BF),
-            vmem((LAYERS, len(hubs), 2 * each, channels), BF),
+            *[vmem((*lead, 2 * each, channels), BF) for lead in landings],
             vmem((LAYERS, CORES, chips, 2 * each, channels), BF),
             pltpu.SemaphoreType.DMA((rows_here,)),
             pltpu.SemaphoreType.DMA((LAYERS,)),
@@ -385,7 +404,7 @@
             pltpu.SemaphoreType.DMA((LAYERS,)),
             pltpu.SemaphoreType.DMA((LAYERS,)),
             pltpu.SemaphoreType.DMA((LAYERS,)),
-            pltpu.SemaphoreType.DMA((LAYERS, len(hubs))),
+            pltpu.SemaphoreType.DMA((LAYERS, max(lead[0] for lead in landings[2::3]))),
             pltpu.SemaphoreType.DMA((LAYERS,)),
             pltpu.SemaphoreType.DMA((LAYERS,)),
             pltpu.SemaphoreType.DMA((LAYERS, chips)),

time: 108 us -> 99.5 us (0.921)
  Pallas kernels: 107 us -> 98.6 us
    pallas_call x1, Pallas kernels: 107 us -> 98.6 us  [per_device(): pl.pallas_call(kernel, name='operator', out_shape=jax.ShapeDtypeStruct((r...]
where the time goes in v3:
time: 99.5 us; the launch traced here: 99.4 us
  Pallas kernels  98.6 us (99%)
    pallas_call x1, Pallas kernels, per_device(): pl.pallas_call(kernel, name='operator', out_shape=jax.ShapeDtypeStruct((r...  98.6 us

profile of v3, /device:TPU:37, one launch (start us, length us, event | category | flops | bytes accessed | tf_op | source)
XLA Modules:
  0.0 99.4 jit_solution(4862933219250893433)
XLA Ops:
  0.0 98.6 %operator.1 = bf16[6,20,1152]{2,1,0:T(8,128)(2,1)S(1)} custom-call(bf16[6,1152,256]{2,1,0:T(8,128)(2,1)} %x_hbm.1, bf16[2,4,2,256,256]{4,3,2,1,0:T(8,128)(2,1)} %sw_hbm.1, bf16[2,256,256]{2,1,0:T(8,128)(2,1)} %lw_hbm.1, bf16[2,256]{1,0:T(2,128)(2,1)} %bias_hbm.1, bf16[256,256]{1,0:T(8,128)(2,1)} %rh_hbm.1, bf16[20,256]{1,0:T(8,128)(2,1)} %rf_hbm.1, ...), custom_call_target="tpu_custom_call" | custom-call | tf_op jit(solution)/shard_map/operator/pallas_call | solution.py:379
  98.6 0.7 copy.18

commit v4 on v3

--- a/solution.py
+++ b/solution.py
@@ -91,12 +91,14 @@
 
 def short_routes(chips):
     half = chips // 2
-    quarter = half // 2
-    start = quarter // 2
-    ahead = [d - quarter for d in range(half, start - 1, -1) if d != quarter]
-    behind = [quarter - d for d in range(half - 1, start - 1, -1) if d != quarter]
-    direct = [s * d for d in range(start - 1, 0, -1) for s in (1, -1)]
-    return direct, [(quarter, tuple(ahead)), (-quarter, tuple(behind))]
+    near = half // 4
+    outer = half - near
+    offsets = [s * d for d in range(near, 0, -1) for s in (1, -1)]
+    ahead = tuple(offsets)
+    behind = tuple(w for w in offsets if w > -near)
+    middle = (2, -2, 1, -1)
+    hubs = [(outer, ahead), (-outer, behind), (near + 1, middle), (-near - 1, middle)]
+    return [2, -2, 1, -1], hubs
 
 
 def sending_order(direct, hubs):
@@ -116,7 +118,7 @@
     state, sw, lw, bias, rh, rf, zf, zi, tf, ti, pm, pin, minn, pout, pmt, mout,
     m2, n2, zonal, pw, returned, xsend, xrecv, pbuf, rbuf_0, cbuf_0, hbuf_0, rbuf_1, cbuf_1, hbuf_1, mall,
     in_sem, sw_sem, small_sem, late_sem,
-    xs_sem, xr_sem, rs_send, rs_stage, rs_recv, ag_send, ag_recv, d2_send, d2_recv,
+    xs_sem, xr_sem, rs_send, rs_stage, rs_recv, ag_send, ag_recv, d2_send, d2_recv, chain,
 ):
     rows_here, columns, channels = state.shape
     devices = lax.axis_size("space")
@@ -144,7 +146,7 @@
 
     barrier = pltpu.get_barrier_semaphore()
 
-    closest = max(abs(d) for hub, window in plans[0][1] for d in (hub, *window))
+    closest = max(abs(d) for _, window in plans[0][1] for d in window)
     greeted = [peer(s * d) for d in range(1, closest + 1) for s in (1, -1)] + [partner]
     for target in greeted:
         pl.semaphore_signal(barrier, inc=1, device_id={"space": target}, device_id_type=MESH)
@@ -162,7 +164,7 @@
         pltpu.make_async_copy(x_hbm.at[h], state.at[h], in_sem.at[h]) for h in range(rows_here)
     ]
     sw_copies = [pltpu.make_async_copy(sw_hbm.at[l], sw.at[l], sw_sem.at[l]) for l in range(LAYERS)]
-    for copy in small_copies + in_copies + late_copies + sw_copies:
+    for copy in small_copies + in_copies:
         copy.start()
 
     for copy in small_copies:
@@ -170,9 +172,20 @@
     spread_f = dot(dot(pm[...], tf[...]).astype(BF), pin[...]) * minn[...].astype(F32)
     m2[...] = spread_f.astype(BF).reshape(m2.shape)
 
+    def pass_word(index):
+        for side in (closest, -closest):
+            pl.semaphore_signal(
+                chain.at[index], inc=1, device_id={"space": peer(side)}, device_id_type=MESH
+            )
+
+    pl.semaphore_wait(barrier, len(greeted))
+    pass_word(0)
+
     for h in range(rows_here):
         in_copies[h].wait()
         zonal[pl.ds(h * 2 * KX, 2 * KX), :] = dot(zf[...], state[h]).astype(BF)
+    for copy in late_copies + sw_copies:
+        copy.start()
 
     def send_partials_to_partner(layer):
         xsend[layer] = dot(m2[other], zonal[...]).astype(BF)
@@ -301,17 +314,18 @@
         modes = mall[layer].astype(F32).reshape(2 * MODES, channels).astype(BF)
         returned[...] = dot(n2[...], modes).astype(BF)
 
+    reduce_sends(0, send_partials_to_partner(0))
+    pl.semaphore_wait(chain.at[0], 2)
+    pass_word(1)
     for copy in late_copies:
         copy.wait()
+    pointwise(0)
+    pl.semaphore_wait(chain.at[1], 2)
+    reduce_hubs(0)
     spread_i = dot(dot(pout[...], ti[...]).astype(BF), pmt[...]) * mout[...].astype(F32)
     n2[...] = spread_i.astype(BF)
     for copy in sw_copies:
         copy.wait()
-    pl.semaphore_wait(barrier, len(greeted))
-
-    reduce_sends(0, send_partials_to_partner(0))
-    pointwise(0)
-    reduce_hubs(0)
     reduce_finish_and_mix(0)
     gather(0)
 
@@ -335,6 +349,8 @@
     gather(1)
 
     half_rh = rh[...] * 0.5
+    spare = jnp.zeros((128 - rf.shape[0], channels), F32)
+    rf_t = jnp.concatenate([rf[...].astype(F32), spare], axis=0).T.astype(BF)
 
     def readout_body(h, carry):
         back = returned[pl.ds(pl.multiple_of(h * 2 * KX, 2 * KX), 2 * KX), :]
@@ -342,10 +358,8 @@
             value = dot(zi[pl.ds(start, size), :], back) + pw[h, pl.ds(start, size), :]
             value = gelu_of_half(value)
             hidden = gelu_of_half(dot(value, half_rh))
-            final = lax.dot_general(
-                rf[...], hidden, (((1,), (1,)), ((), ())), preferred_element_type=F32
-            )
-            out_ref[h, :, pl.ds(start, size)] = final.astype(BF)
+            final = dot(hidden, rf_t)
+            out_ref[h, :, pl.ds(start, size)] = final.T[: rf.shape[0]].astype(BF)
         return carry
 
     lax.fori_loop(0, rows_here, readout_body, 0)
@@ -410,6 +424,7 @@
             pltpu.SemaphoreType.DMA((LAYERS, chips)),
             pltpu.SemaphoreType.DMA((LAYERS,)),
             pltpu.SemaphoreType.DMA((LAYERS,)),
+            pltpu.SemaphoreType.REGULAR((2,)),
         ],
         compiler_params=pltpu.CompilerParams(
             collective_id=0, has_side_effects=True, vmem_limit_bytes=50 * 1024 * 1024

time: 99.5 us -> 97.4 us (0.979)
  Pallas kernels: 98.6 us -> 96.5 us
    pallas_call x1, Pallas kernels: 98.6 us -> 96.5 us  [per_device(): pl.pallas_call(kernel, name='operator', out_shape=jax.ShapeDtypeStruct((r...]
where the time goes in v4:
time: 97.4 us; the launch traced here: 97.3 us
  Pallas kernels  96.5 us (99%)
    pallas_call x1, Pallas kernels, per_device(): pl.pallas_call(kernel, name='operator', out_shape=jax.ShapeDtypeStruct((r...  96.5 us

profile of v4, /device:TPU:37, one launch (start us, length us, event | category | flops | bytes accessed | tf_op | source)
XLA Modules:
  0.0 97.3 jit_solution(5141943397395033435)
XLA Ops:
  0.0 96.5 %operator.1 = bf16[6,20,1152]{2,1,0:T(8,128)(2,1)S(1)} custom-call(bf16[6,1152,256]{2,1,0:T(8,128)(2,1)} %x_hbm.1, bf16[2,4,2,256,256]{4,3,2,1,0:T(8,128)(2,1)} %sw_hbm.1, bf16[2,256,256]{2,1,0:T(8,128)(2,1)} %lw_hbm.1, bf16[2,256]{1,0:T(2,128)(2,1)} %bias_hbm.1, bf16[256,256]{1,0:T(8,128)(2,1)} %rh_hbm.1, bf16[20,256]{1,0:T(8,128)(2,1)} %rf_hbm.1, ...), custom_call_target="tpu_custom_call" | custom-call | tf_op jit(solution)/shard_map/operator/pallas_call | solution.py:393
  96.5 0.7 copy.18

commit v5 on v4

--- a/solution.py
+++ b/solution.py
@@ -135,8 +135,8 @@
     reach = hub_windows[0][1]
     far = [d for d in direct if abs(d) > max(map(abs, hubs))]
     near = [d for d in direct if d not in far]
-    step = 384 if columns % 384 == 0 else columns
-    tiles = [(t * step, step) for t in range(columns // step)]
+    grouped = 3 if rows_here % 3 == 0 else 1
+    read_tiles = [(r, 0, columns) for r in range(grouped)]
 
     def chip_at(distance):
         return lax.rem(chip + distance + chips, chips)
@@ -241,9 +241,7 @@
         half_lw = lw[layer] * 0.5
 
         def body(h, carry):
-            for start, size in tiles:
-                value = dot(state[h, pl.ds(start, size), :], half_lw) + row_bias
-                pw[h, pl.ds(start, size), :] = value
+            pw[h] = dot(state[h], half_lw) + row_bias
             return carry
 
         lax.fori_loop(0, rows_here, body, 0)
@@ -310,9 +308,13 @@
                 relay(arrived(hub + offset))
         for distance in behind[4:] + far[:1]:
             relay(arrived(distance))
+        def back(side):
+            modes = mall[layer, side].astype(F32).reshape(MODES, channels).astype(BF)
+            return dot(n2[side], modes)
+
+        back_own = back(core)
         wait_bytes(mall.at[layer, other], d2_recv.at[layer])
-        modes = mall[layer].astype(F32).reshape(2 * MODES, channels).astype(BF)
-        returned[...] = dot(n2[...], modes).astype(BF)
+        returned[...] = (back_own + back(other)).astype(BF)
 
     reduce_sends(0, send_partials_to_partner(0))
     pl.semaphore_wait(chain.at[0], 2)
@@ -323,21 +325,18 @@
     pl.semaphore_wait(chain.at[1], 2)
     reduce_hubs(0)
     spread_i = dot(dot(pout[...], ti[...]).astype(BF), pmt[...]) * mout[...].astype(F32)
-    n2[...] = spread_i.astype(BF)
+    for side in range(CORES):
+        n2[side] = spread_i[:, side * MODES : (side + 1) * MODES].astype(BF)
     for copy in sw_copies:
         copy.wait()
     reduce_finish_and_mix(0)
     gather(0)
 
     def finish_body(h, carry):
-        back = returned[pl.ds(pl.multiple_of(h * 2 * KX, 2 * KX), 2 * KX), :]
-        part = jnp.zeros((2 * KX, channels), F32)
-        for start, size in tiles:
-            value = dot(zi[pl.ds(start, size), :], back) + pw[h, pl.ds(start, size), :]
-            value = gelu_of_half(value)
-            state[h, pl.ds(start, size), :] = value
-            part = part + dot(zf[:, pl.ds(start, size)], value)
-        zonal[pl.ds(pl.multiple_of(h * 2 * KX, 2 * KX), 2 * KX), :] = part.astype(BF)
+        band = pl.ds(pl.multiple_of(h * 2 * KX, 2 * KX), 2 * KX)
+        value = gelu_of_half(dot(zi[...], returned[band, :]) + pw[h])
+        state[h] = value
+        zonal[band, :] = dot(zf[...], value).astype(BF)
         return carry
 
     lax.fori_loop(0, rows_here, finish_body, 0)
@@ -352,17 +351,35 @@
     spare = jnp.zeros((128 - rf.shape[0], channels), F32)
     rf_t = jnp.concatenate([rf[...].astype(F32), spare], axis=0).T.astype(BF)
 
-    def readout_body(h, carry):
-        back = returned[pl.ds(pl.multiple_of(h * 2 * KX, 2 * KX), 2 * KX), :]
-        for start, size in tiles:
+    def readout_body(group, carry):
+        values, hiddens = {}, {}
+
+        def first(i):
+            r, start, size = read_tiles[i]
+            h = group * grouped + r
+            back = returned[pl.ds(pl.multiple_of(h * 2 * KX, 2 * KX), 2 * KX), :]
             value = dot(zi[pl.ds(start, size), :], back) + pw[h, pl.ds(start, size), :]
-            value = gelu_of_half(value)
-            hidden = gelu_of_half(dot(value, half_rh))
-            final = dot(hidden, rf_t)
-            out_ref[h, :, pl.ds(start, size)] = final.T[: rf.shape[0]].astype(BF)
+            values[i] = gelu_of_half(value)
+
+        def second(i):
+            hiddens[i] = gelu_of_half(dot(values[i], half_rh))
+
+        def third(i):
+            r, start, size = read_tiles[i]
+            final = dot(hiddens[i], rf_t).T[: rf.shape[0]]
+            out_ref[group * grouped + r, :, pl.ds(start, size)] = final.astype(BF)
+
+        count = len(read_tiles)
+        for i in range(count + 2):
+            if i >= 2:
+                third(i - 2)
+            if 1 <= i <= count:
+                second(i - 1)
+            if i < count:
+                first(i)
         return carry
 
-    lax.fori_loop(0, rows_here, readout_body, 0)
+    lax.fori_loop(0, rows_here // grouped, readout_body, 0)
 
     for layer in range(LAYERS):
         wait_bytes(pbuf.at[layer, pl.ds(1, chips - 1)], rs_send.at[layer])
@@ -402,7 +419,7 @@
             like(table_i, 1),
             *[like(a) for a in selections],
             vmem((CORES, MODES, bands), BF),
-            vmem((bands, 2 * MODES), BF),
+            vmem((CORES, bands, MODES), BF),
             vmem((bands, channels), BF),
             vmem((rows_here, columns, channels), F32),
             vmem((bands, channels), BF),

time: 97.4 us -> 94.3 us (0.968)
  Pallas kernels: 96.5 us -> 93.4 us
    pallas_call x1, Pallas kernels: 96.5 us -> 93.4 us  [per_device(): pl.pallas_call(kernel, name='operator', out_shape=jax.ShapeDtypeStruct((r...]
where the time goes in v5:
time: 94.3 us; the launch traced here: 94.1 us
  Pallas kernels  93.4 us (99%)
    pallas_call x1, Pallas kernels, per_device(): pl.pallas_call(kernel, name='operator', out_shape=jax.ShapeDtypeStruct((r...  93.4 us

profile of v5, /device:TPU:37, one launch (start us, length us, event | category | flops | bytes accessed | tf_op | source)
XLA Modules:
  0.0 94.1 jit_solution(10144147648078733785)
XLA Ops:
  0.0 93.4 %operator.1 = bf16[6,20,1152]{2,1,0:T(8,128)(2,1)S(1)} custom-call(bf16[6,1152,256]{2,1,0:T(8,128)(2,1)} %x_hbm.1, bf16[2,4,2,256,256]{4,3,2,1,0:T(8,128)(2,1)} %sw_hbm.1, bf16[2,256,256]{2,1,0:T(8,128)(2,1)} %lw_hbm.1, bf16[2,256]{1,0:T(2,128)(2,1)} %bias_hbm.1, bf16[256,256]{1,0:T(8,128)(2,1)} %rh_hbm.1, bf16[20,256]{1,0:T(8,128)(2,1)} %rf_hbm.1, ...), custom_call_target="tpu_custom_call" | custom-call | tf_op jit(solution)/shard_map/operator/pallas_call | solution.py:410
  93.4 0.7 copy.18
